TPU v7x, 32 devices: a whole 2x2x4 slice. The times are simulated.
32 devices in a mesh: dp: 8 (over z, x), mp: 4 (over y, core).
Axes of the slice: x: 2, y: 2, z: 4, core: 2. Of those that a mesh axis runs over, the one named last changes fastest.
Arguments:
- acts: bfloat16 [1, 16384, 4096], P(None, 'dp'), may hold values from -64 to 64
- out_grads: bfloat16 [1, 16384, 4096], P(None, 'dp', 'mp'), may hold values from -80 to 80
- clip_bound: float32 [1], replicated, may hold values from 163840 to 491520
- noise: float32 [1, 4096, 4096], P(None, 'dp', 'mp'), may hold values from -6 to 6
Outputs:
- update: float32 [1, 4096, 4096], P(None, 'dp', 'mp')
All inputs are finite; a program needn't handle non-finite values.
Results may differ from a plain program's by a relative error of at most 0.0017.
Values may be sent and summed in bfloat16 or wider, within the bound.
A program may use at most 128 MiB of HBM per device.

v0:
```python
import functools
import math

import jax
import jax.numpy as jnp
from jax import lax
from jax.experimental import pallas as pl
from jax.experimental.pallas import tpu as pltpu
from jax.sharding import PartitionSpec as P

SEQ = 512
NT = (((1,), (1,)), ((), ()))
MESH = pl.DeviceIdType.MESH
LIFT = 2.0**50


def coded(value):
    lifted = value * LIFT
    return (lifted * jnp.abs(lifted)).astype(jnp.bfloat16)


def decoded(code):
    code = code.astype(jnp.float32)
    return code * lax.rsqrt(jnp.maximum(jnp.abs(code), 1e-37)) * (1.0 / LIFT)


def kernel(
    groups, lanes, acts_hbm, grads_hbm, bound_ref, out_hbm,
    acts, grads, grads_t, xs, xr, zs, zr, norm_mine, norm_peer, total, out,
    load_sem, out_sem, norm_send, norm_recv, x_send, x_recv, z_send, z_recv,
):
    planes = groups // 2
    steps = 2 * planes
    feats = acts.shape[1] // groups
    half_cols = grads.shape[1] // 2
    examples = acts.shape[0] // SEQ
    me = lax.axis_index("dp")
    lane = lax.axis_index("mp")
    line, pair = me // 2, me % 2
    has_below = (line > 0).astype(jnp.int32)
    has_above = (line < planes - 1).astype(jnp.int32)
    x_peer = {"dp": line * 2 + 1 - pair}
    above = {"dp": jnp.minimum(line + 1, planes - 1) * 2 + pair}
    below = {"dp": jnp.maximum(line - 1, 0) * 2 + pair}

    def rows_of(e):
        return pl.ds(pl.multiple_of(e * SEQ, SEQ), SEQ)

    def load(e, which):
        source, target = (grads_hbm, grads) if which else (acts_hbm, acts)
        return pltpu.make_async_copy(
            source.at[rows_of(e)], target.at[rows_of(e)], load_sem.at[which, e]
        )

    for e in range(examples):
        load(e, 1).start()
        load(e, 0).start()

    barrier = pltpu.get_barrier_semaphore()
    pl.semaphore_signal(barrier, inc=1, device_id=x_peer, device_id_type=MESH)
    for j in range(1, lanes):
        pl.semaphore_signal(
            barrier, inc=1, device_id={"mp": lax.rem(lane + j, lanes)}, device_id_type=MESH
        )

    @pl.when(line > 0)
    def _():
        pl.semaphore_signal(barrier, inc=1, device_id=below, device_id_type=MESH)

    @pl.when(line < planes - 1)
    def _():
        pl.semaphore_signal(barrier, inc=1, device_id=above, device_id_type=MESH)

    cut = SEQ // 2

    def gram(ref, e):
        base = pl.multiple_of(e * SEQ, SEQ)
        low, high = ref[pl.ds(base, cut), :], ref[pl.ds(base + cut, cut), :]
        dot = functools.partial(
            lax.dot_general, dimension_numbers=NT, preferred_element_type=jnp.float32
        )
        return dot(low, low), dot(low, high), dot(high, high)

    def norm_step(e, carry):
        load(e, 1).wait()
        gg = gram(grads, e)
        load(e, 0).wait()
        ga = gram(acts, e)
        prod = ga[0] * gg[0] + 2.0 * (ga[1] * gg[1]) + ga[2] * gg[2]
        norm_mine[e] = jnp.broadcast_to(jnp.sum(prod, keepdims=True), norm_mine.shape[1:])
        return carry

    lax.fori_loop(0, examples, norm_step, 0)
    pl.semaphore_wait(barrier, lanes + has_below + has_above)

    def norm_copy(j):
        return pltpu.make_async_remote_copy(
            src_ref=norm_mine, dst_ref=norm_peer.at[j - 1],
            send_sem=norm_send.at[j - 1], recv_sem=norm_recv.at[j - 1],
            device_id={"mp": lax.rem(lane + j, lanes)}, device_id_type=MESH,
        )

    for j in range(1, lanes):
        norm_copy(j).start()
    for j in range(1, lanes):
        norm_copy(j).wait()

    bound = bound_ref[0]

    def scale_step(e, carry):
        norm_sq = norm_mine[e]
        for j in range(1, lanes):
            norm_sq = norm_sq + norm_peer[j - 1, e]
        factor = (jnp.minimum(1.0, bound / jnp.sqrt(norm_sq + 1e-06)) / bound)[:1, :1]
        scaled = (grads[rows_of(e), :].astype(jnp.float32) * factor).astype(jnp.bfloat16)
        grads_t[:, rows_of(e)] = scaled.T
        return carry

    lax.fori_loop(0, examples, scale_step, 0)

    def target_of(k):
        ups = planes - 1 - line
        up_first = jnp.where(k < ups, planes - 1 - k, k - ups)
        down_first = jnp.where(k < line, k, planes - 1 - (k - line))
        ordered = jnp.where(line < planes // 2, up_first, down_first)
        return jnp.where(k == planes - 1, line, ordered)

    def term(block, half):
        cols = pl.ds(pl.multiple_of(block * feats, feats), feats)
        rows = pl.ds(pl.multiple_of(half * half_cols, half_cols), half_cols)
        return jnp.dot(grads_t[rows, :], acts[:, cols], preferred_element_type=jnp.float32)

    def x_copy(s):
        return pltpu.make_async_remote_copy(
            src_ref=xs.at[s], dst_ref=xr.at[s], send_sem=x_send.at[s], recv_sem=x_recv.at[s],
            device_id=x_peer, device_id_type=MESH,
        )

    def z_copy(s, slot, device):
        return pltpu.make_async_remote_copy(
            src_ref=zs.at[s], dst_ref=zr.at[slot], send_sem=z_send.at[s],
            recv_sem=z_recv.at[slot], device_id=device, device_id_type=MESH,
        )

    def send_step(s, carry):
        xs[s] = coded(term(target_of(s // 2) * 2 + 1 - pair, s % 2))
        x_copy(s).start()
        return carry

    lax.fori_loop(0, steps, send_step, 0)

    def add_arrival(slot):
        z_copy(0, slot, above).wait_recv()
        total[...] += decoded(zr[slot])

    def sum_step(s, carry):
        target, half = target_of(s // 2), s % 2
        slot = target * 2 + half
        own = term(target * 2 + pair, half)
        x_copy(s).wait_recv()
        total[...] = own + decoded(xr[s])

        @pl.when((target >= line) & (line > 0))
        def _():
            add_arrival(slot)

        @pl.when((target < line) & (line < planes - 1))
        def _():
            add_arrival(slot)

        @pl.when((target == line) & (line < planes - 1))
        def _():
            add_arrival(steps + half)

        @pl.when(target > line)
        def _():
            zs[s] = coded(total[...])
            z_copy(s, slot, above).start()

        @pl.when(target < line)
        def _():
            zs[s] = coded(total[...])
            z_copy(s, jnp.where(target == line - 1, steps + half, slot), below).start()

        @pl.when(target == line)
        def _():
            cols = pl.ds(pl.multiple_of(half * half_cols, half_cols), half_cols)
            out[:, cols] = total[...].T
            pltpu.make_async_copy(out.at[:, cols], out_hbm.at[:, cols], out_sem.at[half]).start()

        return carry

    lax.fori_loop(0, steps, sum_step, 0)

    def drain_step(s, carry):
        x_copy(s).wait_send()

        @pl.when(s < steps - 2)
        def _():
            z_copy(s, 0, above).wait_send()

        return carry

    lax.fori_loop(0, steps, drain_step, 0)
    for half in range(2):
        cols = pl.ds(half * half_cols, half_cols)
        pltpu.make_async_copy(out.at[:, cols], out_hbm.at[:, cols], out_sem.at[half]).wait()


def clipped_sum(act_block, grad_block, bound):
    groups, lanes = lax.axis_size("dp"), lax.axis_size("mp")
    tokens, width = act_block.shape
    cols = grad_block.shape[1]
    feats = width // groups
    steps = groups
    examples = tokens // SEQ
    half = (cols // 2, feats)
    dma = pltpu.SemaphoreType.DMA
    any_space = pl.BlockSpec(memory_space=pl.ANY)
    return pl.pallas_call(
        functools.partial(kernel, groups, lanes),
        out_shape=jax.ShapeDtypeStruct((feats, cols), jnp.float32),
        in_specs=[any_space, any_space, pl.BlockSpec(memory_space=pltpu.SMEM)],
        out_specs=any_space,
        scratch_shapes=[
            pltpu.VMEM((tokens, width), jnp.bfloat16),
            pltpu.VMEM((tokens, cols), jnp.bfloat16),
            pltpu.VMEM((cols, tokens), jnp.bfloat16),
            pltpu.VMEM((steps,) + half, jnp.bfloat16),
            pltpu.VMEM((steps,) + half, jnp.bfloat16),
            pltpu.VMEM((steps,) + half, jnp.bfloat16),
            pltpu.VMEM((steps + 2,) + half, jnp.bfloat16),
            pltpu.VMEM((examples, 8, 128), jnp.float32),
            pltpu.VMEM((max(lanes - 1, 1), examples, 8, 128), jnp.float32),
            pltpu.VMEM(half, jnp.float32),
            pltpu.VMEM((feats, cols), jnp.float32),
            dma((2, examples)),
            dma((2,)),
            dma((max(lanes - 1, 1),)),
            dma((max(lanes - 1, 1),)),
            dma((steps,)),
            dma((steps,)),
            dma((steps,)),
            dma((steps + 2,)),
        ],
        compiler_params=pltpu.CompilerParams(
            collective_id=0, has_side_effects=True, vmem_limit_bytes=60 * 2**20
        ),
        name="clipped_sum",
    )(act_block, grad_block, bound)


def on_device(acts, out_grads, clip_bound, noise):
    model_width = acts.shape[2]
    batch_total = acts.shape[1] // SEQ * lax.axis_size("dp")
    out_factor = model_width / math.sqrt(batch_total)
    updates = [
        clipped_sum(acts[g], out_grads[g], clip_bound[g : g + 1]) * out_factor + noise[g]
        for g in range(acts.shape[0])
    ]
    return jnp.stack(updates)


def solution(mesh):
    placed = (P(None, "dp", None), P(None, "dp", "mp"), P(), P(None, "dp", "mp"))
    return jax.shard_map(
        on_device, mesh=mesh, in_specs=placed, out_specs=P(None, "dp", "mp"), check_vma=False
    )
```

profile of v0, /device:TPU:0, one launch (start us, length us, event | category | flops | bytes accessed | tf_op | source)
XLA Modules:
  0.0 122.5 jit_solution(14583100408464639974)
XLA Ops:
  0.7 0.0 copy-start
  0.7 118.3 %clipped_sum.1 = f32[512,1024]{1,0:T(8,128)} custom-call(bf16[2048,4096]{1,0:T(8,128)(2,1)} %bitcast.8, bf16[2048,1024]{1,0:T(8,128)(2,1)} %bitcast.9, f32[1]{0:T(128)S(6)} %copy.5.bound_ref), custom_call_target="tpu_custom_call" | custom-call | tf_op jit(solution)/shard_map/clipped_sum/pallas_call | solution.py:220
  119.0 0.0 copy-done
  119.0 3.5 %fusion = f32[1,512,1024]{2,1,0:T(8,128)} fusion(f32[1,512,1024]{2,1,0:T(8,128)S(1)} %copy-done, f32[512,1024]{1,0:T(8,128)} %clipped_sum.1), kind=kLoop, calls=%fused_computation.1 | loop fusion | flops 1048576 | bytes 6291456 | tf_op jit(solution)/shard_map/stack | solution.py:261
Async XLA Ops:
  0.7 118.3 %copy-start = (f32[1,512,1024]{2,1,0:T(8,128)S(1)}, f32[1,512,1024]{2,1,0:T(8,128)}, u32[]{:S(2)}) copy-start(f32[1,512,1024]{2,1,0:T(8,128)} %param.7) | copy-start | bytes 6291460
where the time goes:
time: 123 us
  Pallas kernels  118 us (96%)
  other arithmetic  3.53 us (3%)
    pallas_call x1, Pallas kernels, clipped_sum(): pl.pallas_call(functools.partial(kernel, groups, lanes), out_shape=jax.Sh...  118 us
    another operation x1, other arithmetic, on_device(): return jnp.stack(updates)  3.53 us

commit v1 on v0

v1 whole, which is shorter than its diff:
```python
import functools
import math

import jax
import jax.numpy as jnp
from jax import lax
from jax.experimental import pallas as pl
from jax.experimental.pallas import tpu as pltpu
from jax.sharding import PartitionSpec as P

SEQ = 512
PIECES = 4
NT = (((1,), (1,)), ((), ()))
MESH = pl.DeviceIdType.MESH
LIFT = 2.0**50


def coded(value):
    lifted = value * LIFT
    return (lifted * jnp.abs(lifted)).astype(jnp.bfloat16)


def decoded(code):
    code = code.astype(jnp.float32)
    return code * lax.rsqrt(jnp.maximum(jnp.abs(code), 1e-37)) * (1.0 / LIFT)


def kernel(
    groups, lanes, share, acts_hbm, grads_hbm, bound_ref, out_hbm,
    acts, grads, grads_t, xs, xr, zs, zr, fr, gram_mine, gram_peer, norm_mine, norm_peer, total, out,
    load_sem, out_sem, gram_send, gram_recv, norm_send, norm_recv,
    x_send, x_recv, z_send, z_recv, f_send, f_recv,
):
    planes = groups // 2
    last = planes - 1
    feats = acts.shape[1] // groups
    width = grads.shape[1] // PIECES
    examples = acts.shape[0] // SEQ
    owned = examples // share
    me = lax.axis_index("dp")
    lane = lax.axis_index("mp")
    line, pair = me // 2, me % 2
    x_peer = {"dp": line * 2 + 1 - pair}
    above = {"dp": jnp.minimum(line + 1, last) * 2 + pair}
    below = {"dp": jnp.maximum(line - 1, 0) * 2 + pair}
    has_below = (line > 0).astype(jnp.int32)
    has_above = (line < last).astype(jnp.int32)
    part = lane % share
    first = part * owned
    away = (first + owned) % examples

    def example(i):
        return lax.rem(away + i, examples)

    def rows_of(e):
        return pl.ds(pl.multiple_of(e * SEQ, SEQ), SEQ)

    def load(e, which):
        source, target = (grads_hbm, grads) if which else (acts_hbm, acts)
        return pltpu.make_async_copy(
            source.at[rows_of(e)], target.at[rows_of(e)], load_sem.at[which, e]
        )

    for i in range(examples):
        load(example(i), 1).start()
    for i in range(examples - owned, examples):
        load(example(i), 0).start()
    for i in range(examples - owned):
        load(example(i), 0).start()

    barrier = pltpu.get_barrier_semaphore()
    pl.semaphore_signal(barrier, inc=1, device_id=x_peer, device_id_type=MESH)
    for j in range(1, lanes):
        pl.semaphore_signal(
            barrier, inc=1, device_id={"mp": lax.rem(lane + j, lanes)}, device_id_type=MESH
        )

    @pl.when(line > 0)
    def _():
        pl.semaphore_signal(barrier, inc=1, device_id=below, device_id_type=MESH)

    @pl.when(line < last)
    def _():
        pl.semaphore_signal(barrier, inc=1, device_id=above, device_id_type=MESH)

    cut = SEQ // 2

    def gram(ref, e):
        base = pl.multiple_of(e * SEQ, SEQ)
        low, high = ref[pl.ds(base, cut), :], ref[pl.ds(base + cut, cut), :]
        dot = functools.partial(
            lax.dot_general, dimension_numbers=NT, preferred_element_type=jnp.float32
        )
        return dot(low, low), dot(low, high), dot(high, high)

    def gram_copy(i):
        mate = lane - part + lax.rem(part + 1, share)
        return pltpu.make_async_remote_copy(
            src_ref=gram_mine.at[i], dst_ref=gram_peer.at[i],
            send_sem=gram_send.at[i], recv_sem=gram_recv.at[i],
            device_id={"mp": mate}, device_id_type=MESH,
        )

    if share > 1:
        def away_step(i, carry):
            e = example(i)
            load(e, 1).wait()
            for j, block in enumerate(gram(grads, e)):
                gram_mine[i, j] = block
            norm_mine[e] = jnp.zeros(norm_mine.shape[1:], jnp.float32)
            return carry

        lax.fori_loop(0, owned, away_step, 0)

    pl.semaphore_wait(barrier, lanes + has_below + has_above)
    if share > 1:
        for i in range(owned):
            gram_copy(i).start()

    def norm_step(i, carry):
        e = first + i
        load(e, 1).wait()
        gg = gram(grads, e)
        load(e, 0).wait()
        ga = gram(acts, e)
        if share > 1:
            gram_copy(i).wait_recv()
            gg = tuple(gg[j] + gram_peer[i, j] for j in range(3))
        prod = ga[0] * gg[0] + 2.0 * (ga[1] * gg[1]) + ga[2] * gg[2]
        norm_mine[e] = jnp.broadcast_to(jnp.sum(prod, keepdims=True), norm_mine.shape[1:])
        return carry

    lax.fori_loop(0, owned, norm_step, 0)

    def norm_copy(j):
        return pltpu.make_async_remote_copy(
            src_ref=norm_mine, dst_ref=norm_peer.at[j - 1],
            send_sem=norm_send.at[j - 1], recv_sem=norm_recv.at[j - 1],
            device_id={"mp": lax.rem(lane + j, lanes)}, device_id_type=MESH,
        )

    for j in range(1, lanes):
        norm_copy(j).start()

    def turn_step(e, carry):
        grads_t[:, rows_of(e)] = grads[rows_of(e), :].T
        return carry

    lax.fori_loop(0, examples, turn_step, 0)
    for i in range(examples - owned):
        load(example(i), 0).wait()
    for j in range(1, lanes):
        norm_copy(j).wait()
    if share > 1:
        for i in range(owned):
            gram_copy(i).wait_send()

    bound = bound_ref[0]
    factors = []
    for e in range(examples):
        norm_sq = norm_mine[e]
        for j in range(1, lanes):
            norm_sq = norm_sq + norm_peer[j - 1, e]
        factors.append((jnp.minimum(1.0, bound / jnp.sqrt(norm_sq + 1e-06)) / bound)[:1, :1])

    def cols_of(q):
        return pl.ds(pl.multiple_of(q * width, width), width)

    def scale(q):
        for e in range(examples):
            at = (cols_of(q), pl.ds(e * SEQ, SEQ))
            grads_t[at] = (grads_t[at].astype(jnp.float32) * factors[e]).astype(jnp.bfloat16)

    def sends_far(p):
        edge = (p == 0) | (p == last)
        up = (p < last) & ((p == 0) | (2 * p >= planes))
        down = (p > 0) & ((p == last) | (2 * p < planes))
        return up, down, jnp.where(edge, PIECES // 2, PIECES)

    far_up, far_down, far_count = sends_far(line)
    far_target = jnp.where(far_up, line + 1, line - 1)
    far_count = jnp.where(far_up | far_down, far_count, 0)

    def is_far(t, q):
        return (t == far_target) & (q < far_count)

    def arrivals_far(side, q):
        p = line - 1 if side == 0 else line + 1
        up, down, count = sends_far(p)
        exists = (line > 0) & up if side == 0 else (line < last) & down
        return exists & (q < count)

    def slot_of(t, q):
        return t * PIECES + q

    def term(block, q):
        cols = pl.ds(pl.multiple_of(block * feats, feats), feats)
        return jnp.dot(grads_t[cols_of(q), :], acts[:, cols], preferred_element_type=jnp.float32)

    def x_copy(s):
        return pltpu.make_async_remote_copy(
            src_ref=xs.at[s], dst_ref=xr.at[s], send_sem=x_send.at[s], recv_sem=x_recv.at[s],
            device_id=x_peer, device_id_type=MESH,
        )

    def z_copy(s, slot, device):
        return pltpu.make_async_remote_copy(
            src_ref=zs.at[s], dst_ref=zr.at[slot], send_sem=z_send.at[s],
            recv_sem=z_recv.at[slot], device_id=device, device_id_type=MESH,
        )

    def far_copy(q, side):
        slot = side * PIECES + q
        return pltpu.make_async_remote_copy(
            src_ref=xs.at[slot_of(far_target, q)], dst_ref=fr.at[slot], send_sem=f_send.at[q],
            recv_sem=f_recv.at[slot], device_id={"dp": far_target * 2 + pair}, device_id_type=MESH,
        )

    def target_of(k):
        ups = last - line
        up_first = jnp.where(k < ups, last - k, k - ups)
        down_first = jnp.where(k < line, k, last - (k - line))
        return jnp.where(2 * line < planes, up_first, down_first)

    def start_step(s, carry):
        @pl.when(s < PIECES)
        def _():
            scale(s)

        t, q = target_of(s // PIECES), s % PIECES

        @pl.when(jnp.logical_not(is_far(t, q)))
        def _():
            xs[slot_of(t, q)] = coded(term(t * 2 + 1 - pair, q))
            x_copy(slot_of(t, q)).start()

        @pl.when(s < far_count)
        def _():
            xs[slot_of(far_target, s)] = coded(term(far_target * 2 + 1 - pair, s))
            far_copy(s, jnp.where(far_up, 0, 1)).start()

        return carry

    lax.fori_loop(0, last * PIECES, start_step, 0)

    def pass_on(t, q, up):
        slot = slot_of(t, q)
        total[...] = term(t * 2 + pair, q)

        @pl.when(jnp.logical_not(is_far(t, q)))
        def _():
            x_copy(slot).wait_recv()
            total[...] += decoded(xr[slot])

        @pl.when(line > 0 if up else line < last)
        def _():
            z_copy(0, slot, above).wait_recv()
            total[...] += decoded(zr[slot])

        zs[slot] = coded(total[...])
        if up:
            z_copy(slot, slot, above).start()
        else:
            z_copy(slot, jnp.where(t == line - 1, planes * PIECES + q, slot), below).start()

    def pass_step(s, carry):
        i, j, k = s - line, s - (last - line), s - 2

        @pl.when((i >= 0) & (i < (last - line) * PIECES))
        def _():
            pass_on(last - i // PIECES, i % PIECES, True)

        @pl.when((j >= 0) & (j < line * PIECES))
        def _():
            pass_on(j // PIECES, j % PIECES, False)

        @pl.when((k >= 0) & (k < PIECES))
        def _():
            total[...] = term(line * 2 + 1 - pair, k)
            for side in range(2):
                @pl.when(arrivals_far(side, k))
                def _():
                    far_copy(k, side).wait_recv()
                    total[...] += decoded(fr[side * PIECES + k])

            slot = slot_of(line, k)
            xs[slot] = coded(total[...])
            x_copy(slot).start()

        return carry

    lax.fori_loop(0, max(last * PIECES, PIECES + 2), pass_step, 0)

    def out_copy(q):
        return pltpu.make_async_copy(
            out.at[:, cols_of(q)], out_hbm.at[:, cols_of(q)], out_sem.at[q]
        )

    def final_step(q, carry):
        slot = slot_of(line, q)
        total[...] = term(line * 2 + pair, q)

        @pl.when(line > 0)
        def _():
            z_copy(0, slot, above).wait_recv()
            total[...] += decoded(zr[slot])

        @pl.when(line < last)
        def _():
            z_copy(0, planes * PIECES + q, above).wait_recv()
            total[...] += decoded(zr[planes * PIECES + q])

        x_copy(slot).wait_recv()
        out[:, cols_of(q)] = (total[...] + decoded(xr[slot])).T
        out_copy(q).start()
        return carry

    lax.fori_loop(0, PIECES, final_step, 0)

    def drain_step(s, carry):
        t, q = s // PIECES, s % PIECES
        far = is_far(t, q)

        @pl.when(far)
        def _():
            far_copy(q, 0).wait_send()

        @pl.when(jnp.logical_not(far))
        def _():
            x_copy(s).wait_send()

        @pl.when(t != line)
        def _():
            z_copy(s, 0, above).wait_send()

        return carry

    lax.fori_loop(0, planes * PIECES, drain_step, 0)
    for q in range(PIECES):
        out_copy(q).wait()


def clipped_sum(act_block, grad_block, bound):
    groups, lanes = lax.axis_size("dp"), lax.axis_size("mp")
    tokens, width = act_block.shape
    cols = grad_block.shape[1]
    feats = width // groups
    slots = groups // 2 * PIECES
    examples = tokens // SEQ
    share = 2 if lanes % 2 == 0 and examples % 2 == 0 else 1
    piece = (cols // PIECES, feats)
    grams = (examples // share if share > 1 else 1, 3, SEQ // 2, SEQ // 2)
    dma = pltpu.SemaphoreType.DMA
    any_space = pl.BlockSpec(memory_space=pl.ANY)
    return pl.pallas_call(
        functools.partial(kernel, groups, lanes, share),
        out_shape=jax.ShapeDtypeStruct((feats, cols), jnp.float32),
        in_specs=[any_space, any_space, pl.BlockSpec(memory_space=pltpu.SMEM)],
        out_specs=any_space,
        scratch_shapes=[
            pltpu.VMEM((tokens, width), jnp.bfloat16),
            pltpu.VMEM((tokens, cols), jnp.bfloat16),
            pltpu.VMEM((cols, tokens), jnp.bfloat16),
            pltpu.VMEM((slots,) + piece, jnp.bfloat16),
            pltpu.VMEM((slots,) + piece, jnp.bfloat16),
            pltpu.VMEM((slots,) + piece, jnp.bfloat16),
            pltpu.VMEM((slots + PIECES,) + piece, jnp.bfloat16),
            pltpu.VMEM((2 * PIECES,) + piece, jnp.bfloat16),
            pltpu.VMEM(grams, jnp.float32),
            pltpu.VMEM(grams, jnp.float32),
            pltpu.VMEM((examples, 8, 128), jnp.float32),
            pltpu.VMEM((max(lanes - 1, 1), examples, 8, 128), jnp.float32),
            pltpu.VMEM(piece, jnp.float32),
            pltpu.VMEM((feats, cols), jnp.float32),
            dma((2, examples)),
            dma((PIECES,)),
            dma((grams[0],)),
            dma((grams[0],)),
            dma((max(lanes - 1, 1),)),
            dma((max(lanes - 1, 1),)),
            dma((slots,)),
            dma((slots,)),
            dma((slots,)),
            dma((slots + PIECES,)),
            dma((PIECES,)),
            dma((2 * PIECES,)),
        ],
        compiler_params=pltpu.CompilerParams(
            collective_id=0, has_side_effects=True, vmem_limit_bytes=60 * 2**20
        ),
        name="clipped_sum",
    )(act_block, grad_block, bound)


def on_device(acts, out_grads, clip_bound, noise):
    model_width = acts.shape[2]
    batch_total = acts.shape[1] // SEQ * lax.axis_size("dp")
    out_factor = model_width / math.sqrt(batch_total)
    updates = [
        clipped_sum(acts[g], out_grads[g], clip_bound[g : g + 1]) * out_factor + noise[g]
        for g in range(acts.shape[0])
    ]
    return jnp.stack(updates)


def solution(mesh):
    placed = (P(None, "dp", None), P(None, "dp", "mp"), P(), P(None, "dp", "mp"))
    return jax.shard_map(
        on_device, mesh=mesh, in_specs=placed, out_specs=P(None, "dp", "mp"), check_vma=False
    )
```

time: 123 us -> 104 us (0.85)
  Pallas kernels: 118 us -> 99.3 us
    pallas_call x1, Pallas kernels: 118 us -> 99.3 us  [clipped_sum(): pl.pallas_call(functools.partial(kernel, groups, lanes, share), out_shape...]
where the time goes in v1:
time: 104 us; the launch traced here: 103 us
  Pallas kernels  99.3 us (95%)
  other arithmetic  3.53 us (3%)
    pallas_call x1, Pallas kernels, clipped_sum(): pl.pallas_call(functools.partial(kernel, groups, lanes, share), out_shape...  99.3 us
    another operation x1, other arithmetic, on_device(): return jnp.stack(updates)  3.53 us

profile of v1, /device:TPU:0, one launch (start us, length us, event | category | flops | bytes accessed | tf_op | source)
XLA Modules:
  0.0 103.5 jit_solution(5070911847870685014)
XLA Ops:
  0.7 0.0 copy-start
  0.7 99.3 %clipped_sum.1 = f32[512,1024]{1,0:T(8,128)} custom-call(bf16[2048,4096]{1,0:T(8,128)(2,1)} %bitcast.8, bf16[2048,1024]{1,0:T(8,128)(2,1)} %bitcast.9, f32[1]{0:T(128)S(6)} %copy.5.bound_ref), custom_call_target="tpu_custom_call" | custom-call | tf_op jit(solution)/shard_map/clipped_sum/pallas_call | solution.py:355
  99.9 0.0 copy-done
  99.9 3.5 %fusion = f32[1,512,1024]{2,1,0:T(8,128)} fusion(f32[1,512,1024]{2,1,0:T(8,128)S(1)} %copy-done, f32[512,1024]{1,0:T(8,128)} %clipped_sum.1), kind=kLoop, calls=%fused_computation.1 | loop fusion | flops 1048576 | bytes 6291456 | tf_op jit(solution)/shard_map/stack | solution.py:403
Async XLA Ops:
  0.7 99.3 %copy-start = (f32[1,512,1024]{2,1,0:T(8,128)S(1)}, f32[1,512,1024]{2,1,0:T(8,128)}, u32[]{:S(2)}) copy-start(f32[1,512,1024]{2,1,0:T(8,128)} %param.7) | copy-start | bytes 6291460

commit v2 on v1

--- a/solution.py
+++ b/solution.py
@@ -10,6 +10,7 @@
 
 SEQ = 512
 PIECES = 4
+AHEAD = PIECES
 NT = (((1,), (1,)), ((), ()))
 MESH = pl.DeviceIdType.MESH
 LIFT = 2.0**50
@@ -26,9 +27,9 @@
 
 
 def kernel(
-    groups, lanes, share, acts_hbm, grads_hbm, bound_ref, out_hbm,
-    acts, grads, grads_t, xs, xr, zs, zr, fr, gram_mine, gram_peer, norm_mine, norm_peer, total, out,
-    load_sem, out_sem, gram_send, gram_recv, norm_send, norm_recv,
+    groups, lanes, share, out_factor, acts_hbm, grads_hbm, bound_ref, noise_hbm, out,
+    acts, grads, grads_t, xs, xr, zs, zr, fr, gram_mine, gram_peer, gram_kept, gram_own, parts, norm_mine, norm_peer, total, noise,
+    load_sem, noise_sem, gram_send, gram_recv, norm_send, norm_recv,
     x_send, x_recv, z_send, z_recv, f_send, f_recv,
 ):
     planes = groups // 2
@@ -63,10 +64,7 @@
 
     for i in range(examples):
         load(example(i), 1).start()
-    for i in range(examples - owned, examples):
-        load(example(i), 0).start()
-    for i in range(examples - owned):
-        load(example(i), 0).start()
+    load(first, 0).start()
 
     barrier = pltpu.get_barrier_semaphore()
     pl.semaphore_signal(barrier, inc=1, device_id=x_peer, device_id_type=MESH)
@@ -82,6 +80,9 @@
     @pl.when(line < last)
     def _():
         pl.semaphore_signal(barrier, inc=1, device_id=above, device_id_type=MESH)
+
+    def turn(e):
+        grads_t[:, rows_of(e)] = grads[rows_of(e), :].T
 
     cut = SEQ // 2
 
@@ -107,30 +108,48 @@
             load(e, 1).wait()
             for j, block in enumerate(gram(grads, e)):
                 gram_mine[i, j] = block
-            norm_mine[e] = jnp.zeros(norm_mine.shape[1:], jnp.float32)
             return carry
 
         lax.fori_loop(0, owned, away_step, 0)
 
+    def own_step(i, carry):
+        load(first + i, 1).wait()
+        for j, block in enumerate(gram(grads, first + i)):
+            gram_own[i, j] = block
+        return carry
+
+    for i in range(1, owned):
+        load(first + i, 0).start()
+    lax.fori_loop(0, owned, own_step, 0)
     pl.semaphore_wait(barrier, lanes + has_below + has_above)
     if share > 1:
         for i in range(owned):
             gram_copy(i).start()
 
-    def norm_step(i, carry):
+    def inner(a, b):
+        prod = a[0] * b[0] + 2.0 * (a[1] * b[1]) + a[2] * b[2]
+        rows = jnp.sum(prod.reshape(cut // 8, 8, cut), axis=0)
+        return sum(rows[:, c : c + 128] for c in range(0, cut, 128))
+
+    late = examples - owned
+    for i in range(owned):
         e = first + i
-        load(e, 1).wait()
-        gg = gram(grads, e)
         load(e, 0).wait()
+        for j in range(i * late // owned, (i + 1) * late // owned):
+            load(example(j), 0).start()
         ga = gram(acts, e)
-        if share > 1:
-            gram_copy(i).wait_recv()
-            gg = tuple(gg[j] + gram_peer[i, j] for j in range(3))
-        prod = ga[0] * gg[0] + 2.0 * (ga[1] * gg[1]) + ga[2] * gg[2]
-        norm_mine[e] = jnp.broadcast_to(jnp.sum(prod, keepdims=True), norm_mine.shape[1:])
-        return carry
-
-    lax.fori_loop(0, owned, norm_step, 0)
+        gg = [gram_own[i, j] for j in range(3)]
+        if share > 1 and i == owned - 1:
+            for k in range(owned):
+                gram_copy(k).wait_recv()
+            gg = [gg[j] + gram_peer[i, j] for j in range(3)]
+        elif share > 1:
+            for j in range(3):
+                gram_kept[i, j] = ga[j]
+        norm_mine[i] = inner(ga, gg)
+    if share > 1:
+        for i in range(owned - 1):
+            norm_mine[i] += inner(gram_kept[i], gram_peer[i])
 
     def norm_copy(j):
         return pltpu.make_async_remote_copy(
@@ -147,29 +166,11 @@
         return carry
 
     lax.fori_loop(0, examples, turn_step, 0)
-    for i in range(examples - owned):
+    for i in range(late):
         load(example(i), 0).wait()
-    for j in range(1, lanes):
-        norm_copy(j).wait()
-    if share > 1:
-        for i in range(owned):
-            gram_copy(i).wait_send()
-
-    bound = bound_ref[0]
-    factors = []
-    for e in range(examples):
-        norm_sq = norm_mine[e]
-        for j in range(1, lanes):
-            norm_sq = norm_sq + norm_peer[j - 1, e]
-        factors.append((jnp.minimum(1.0, bound / jnp.sqrt(norm_sq + 1e-06)) / bound)[:1, :1])
 
     def cols_of(q):
         return pl.ds(pl.multiple_of(q * width, width), width)
-
-    def scale(q):
-        for e in range(examples):
-            at = (cols_of(q), pl.ds(e * SEQ, SEQ))
-            grads_t[at] = (grads_t[at].astype(jnp.float32) * factors[e]).astype(jnp.bfloat16)
 
     def sends_far(p):
         edge = (p == 0) | (p == last)
@@ -197,6 +198,45 @@
         cols = pl.ds(pl.multiple_of(block * feats, feats), feats)
         return jnp.dot(grads_t[cols_of(q), :], acts[:, cols], preferred_element_type=jnp.float32)
 
+    lead = jnp.where(2 * line < planes, last, 0)
+    lead_q = jnp.where(is_far(lead, 0), far_count, 0)
+    openers = ((lead, lead_q), (far_target, 0)) if last > 0 else ()
+    for k, (t, q) in enumerate(openers):
+        for e in range(examples):
+            tokens = pl.ds(e * SEQ, SEQ)
+            cols = pl.ds(pl.multiple_of((t * 2 + 1 - pair) * feats, feats), feats)
+            parts[k, e] = jnp.dot(
+                grads_t[cols_of(q), tokens], acts[tokens, cols], preferred_element_type=jnp.float32
+            )
+
+    noise_copy = pltpu.make_async_copy(noise_hbm, noise, noise_sem)
+    noise_copy.start()
+    for j in range(1, lanes):
+        norm_copy(j).wait()
+
+    bound = bound_ref[0]
+
+    def factor_of(terms):
+        norm_sq = jnp.sum(functools.reduce(jnp.add, terms), keepdims=True)
+        return jnp.minimum(1.0, bound / jnp.sqrt(norm_sq + 1e-06)) / bound
+
+    factors = []
+    for g in range(share):
+        for i in range(owned):
+            same = [norm_mine[i]] + [norm_peer[j - 1, i] for j in range(share, lanes, share)]
+            other = [norm_peer[j - 1, i] for j in range(1, lanes, share)]
+            if share == 1:
+                factors.append(factor_of(same))
+            else:
+                factors.append(factor_of([
+                    jnp.where(part == g, a, b) for a, b in zip(same, other)
+                ]))
+
+    def scale(q):
+        for e in range(examples):
+            at = (cols_of(q), pl.ds(e * SEQ, SEQ))
+            grads_t[at] = (grads_t[at].astype(jnp.float32) * factors[e]).astype(jnp.bfloat16)
+
     def x_copy(s):
         return pltpu.make_async_remote_copy(
             src_ref=xs.at[s], dst_ref=xr.at[s], send_sem=x_send.at[s], recv_sem=x_recv.at[s],
@@ -216,32 +256,46 @@
             recv_sem=f_recv.at[slot], device_id={"dp": far_target * 2 + pair}, device_id_type=MESH,
         )
 
-    def target_of(k):
-        ups = last - line
-        up_first = jnp.where(k < ups, last - k, k - ups)
-        down_first = jnp.where(k < line, k, last - (k - line))
-        return jnp.where(2 * line < planes, up_first, down_first)
+    for k, (t, q) in enumerate(openers):
+        slot = slot_of(t, q)
+        xs[slot] = coded(sum(parts[k, e] * factors[e] for e in range(examples)))
+        if k == 0:
+            x_copy(slot).start()
+        else:
+            far_copy(q, jnp.where(far_up, 0, 1)).start()
+
+    def send_far(t, q):
+        @pl.when(jnp.logical_not(is_far(t, q) | ((t == lead) & (q == lead_q))))
+        def _():
+            xs[slot_of(t, q)] = coded(term(t * 2 + 1 - pair, q))
+            x_copy(slot_of(t, q)).start()
+
+    def each(s, step):
+        i, j = s - line, s - (last - line)
+
+        @pl.when((i >= 0) & (i < (last - line) * PIECES))
+        def _():
+            step(last - i // PIECES, i % PIECES, True)
+
+        @pl.when((j >= 0) & (j < line * PIECES))
+        def _():
+            step(j // PIECES, j % PIECES, False)
 
     def start_step(s, carry):
         @pl.when(s < PIECES)
         def _():
             scale(s)
 
-        t, q = target_of(s // PIECES), s % PIECES
-
-        @pl.when(jnp.logical_not(is_far(t, q)))
-        def _():
-            xs[slot_of(t, q)] = coded(term(t * 2 + 1 - pair, q))
-            x_copy(slot_of(t, q)).start()
-
-        @pl.when(s < far_count)
+        each(s, lambda t, q, up: send_far(t, q))
+
+        @pl.when((s > 0) & (s < far_count))
         def _():
             xs[slot_of(far_target, s)] = coded(term(far_target * 2 + 1 - pair, s))
             far_copy(s, jnp.where(far_up, 0, 1)).start()
 
         return carry
 
-    lax.fori_loop(0, last * PIECES, start_step, 0)
+    lax.fori_loop(0, AHEAD, start_step, 0)
 
     def pass_on(t, q, up):
         slot = slot_of(t, q)
@@ -263,16 +317,13 @@
         else:
             z_copy(slot, jnp.where(t == line - 1, planes * PIECES + q, slot), below).start()
 
+    edge = (line == 0) | (line == last)
+    opens = jnp.maximum(last * PIECES - AHEAD - jnp.where(edge, 0, PIECES), 0)
+
     def pass_step(s, carry):
-        i, j, k = s - line, s - (last - line), s - 2
-
-        @pl.when((i >= 0) & (i < (last - line) * PIECES))
-        def _():
-            pass_on(last - i // PIECES, i % PIECES, True)
-
-        @pl.when((j >= 0) & (j < line * PIECES))
-        def _():
-            pass_on(j // PIECES, j % PIECES, False)
+        k = s - opens
+        each(s + AHEAD, lambda t, q, up: send_far(t, q))
+        each(s, pass_on)
 
         @pl.when((k >= 0) & (k < PIECES))
         def _():
@@ -289,12 +340,9 @@
 
         return carry
 
-    lax.fori_loop(0, max(last * PIECES, PIECES + 2), pass_step, 0)
-
-    def out_copy(q):
-        return pltpu.make_async_copy(
-            out.at[:, cols_of(q)], out_hbm.at[:, cols_of(q)], out_sem.at[q]
-        )
+    lax.fori_loop(0, max(last, 1) * PIECES, pass_step, 0)
+
+    noise_copy.wait()
 
     def final_step(q, carry):
         slot = slot_of(line, q)
@@ -311,8 +359,8 @@
             total[...] += decoded(zr[planes * PIECES + q])
 
         x_copy(slot).wait_recv()
-        out[:, cols_of(q)] = (total[...] + decoded(xr[slot])).T
-        out_copy(q).start()
+        summed = (total[...] + decoded(xr[slot])).T
+        out[:, cols_of(q)] = summed * out_factor + noise[:, cols_of(q)]
         return carry
 
     lax.fori_loop(0, PIECES, final_step, 0)
@@ -336,11 +384,12 @@
         return carry
 
     lax.fori_loop(0, planes * PIECES, drain_step, 0)
-    for q in range(PIECES):
-        out_copy(q).wait()
-
-
-def clipped_sum(act_block, grad_block, bound):
+    if share > 1:
+        for i in range(owned):
+            gram_copy(i).wait_send()
+
+
+def clipped_sum(act_block, grad_block, bound, noise, out_factor):
     groups, lanes = lax.axis_size("dp"), lax.axis_size("mp")
     tokens, width = act_block.shape
     cols = grad_block.shape[1]
@@ -353,10 +402,10 @@
     dma = pltpu.SemaphoreType.DMA
     any_space = pl.BlockSpec(memory_space=pl.ANY)
     return pl.pallas_call(
-        functools.partial(kernel, groups, lanes, share),
-        out_shape=jax.ShapeDtypeStruct((feats, cols), jnp.float32),
-        in_specs=[any_space, any_space, pl.BlockSpec(memory_space=pltpu.SMEM)],
-        out_specs=any_space,
+        functools.partial(kernel, groups, lanes, share, out_factor),
+        out_shape=pltpu.VMEM((feats, cols), jnp.float32),
+        in_specs=[any_space, any_space, pl.BlockSpec(memory_space=pltpu.SMEM), any_space],
+        out_specs=pl.BlockSpec(memory_space=pltpu.VMEM),
         scratch_shapes=[
             pltpu.VMEM((tokens, width), jnp.bfloat16),
             pltpu.VMEM((tokens, cols), jnp.bfloat16),
@@ -368,12 +417,15 @@
             pltpu.VMEM((2 * PIECES,) + piece, jnp.bfloat16),
             pltpu.VMEM(grams, jnp.float32),
             pltpu.VMEM(grams, jnp.float32),
-            pltpu.VMEM((examples, 8, 128), jnp.float32),
-            pltpu.VMEM((max(lanes - 1, 1), examples, 8, 128), jnp.float32),
+            pltpu.VMEM(grams, jnp.float32),
+            pltpu.VMEM((examples // share,) + grams[1:], jnp.float32),
+            pltpu.VMEM((2, examples) + piece, jnp.float32),
+            pltpu.VMEM((examples // share, 8, 128), jnp.float32),
+            pltpu.VMEM((max(lanes - 1, 1), examples // share, 8, 128), jnp.float32),
             pltpu.VMEM(piece, jnp.float32),
             pltpu.VMEM((feats, cols), jnp.float32),
             dma((2, examples)),
-            dma((PIECES,)),
+            dma(()),
             dma((grams[0],)),
             dma((grams[0],)),
             dma((max(lanes - 1, 1),)),
@@ -386,10 +438,10 @@
             dma((2 * PIECES,)),
         ],
         compiler_params=pltpu.CompilerParams(
-            collective_id=0, has_side_effects=True, vmem_limit_bytes=60 * 2**20
+            collective_id=0, has_side_effects=True, vmem_limit_bytes=61 * 2**20
         ),
         name="clipped_sum",
-    )(act_block, grad_block, bound)
+    )(act_block, grad_block, bound, noise)
 
 
 def on_device(acts, out_grads, clip_bound, noise):
@@ -397,7 +449,7 @@
     batch_total = acts.shape[1] // SEQ * lax.axis_size("dp")
     out_factor = model_width / math.sqrt(batch_total)
     updates = [
-        clipped_sum(acts[g], out_grads[g], clip_bound[g : g + 1]) * out_factor + noise[g]
+        clipped_sum(acts[g], out_grads[g], clip_bound[g : g + 1], noise[g], out_factor)
         for g in range(acts.shape[0])
     ]
     return jnp.stack(updates)

time: 104 us -> 98.5 us (0.947)
  other arithmetic: 3.53 us -> 0 us
  Pallas kernels: 99.3 us -> 96.4 us
  local copies, waits for them, and re-layouts: 0.01 us -> 1.32 us
    another operation x1 -> x0, other arithmetic: 3.53 us -> none  [on_device(): return jnp.stack(updates)]
    pallas_call x1, Pallas kernels: 99.3 us -> 96.4 us  [clipped_sum(): pl.pallas_call(functools.partial(kernel, groups, lanes, share, out_factor...]
    unnamed x2 -> x1, local copies, waits for them, and re-layouts: 0.01 us -> 1.32 us
where the time goes in v2:
time: 98.5 us; the launch traced here: 98.3 us
  Pallas kernels  96.4 us (98%)
  local copies, waits for them, and re-layouts  1.32 us (1%)
    pallas_call x1, Pallas kernels, clipped_sum(): pl.pallas_call(functools.partial(kernel, groups, lanes, share, out_factor...  96.4 us

profile of v2, /device:TPU:0, one launch (start us, length us, event | category | flops | bytes accessed | tf_op | source)
XLA Modules:
  0.0 98.3 jit_solution(4416111166113761656)
XLA Ops:
  0.7 96.4 %clipped_sum.1 = f32[512,1024]{1,0:T(8,128)S(1)} custom-call(bf16[2048,4096]{1,0:T(8,128)(2,1)} %bitcast.5, bf16[2048,1024]{1,0:T(8,128)(2,1)} %bitcast.6, f32[1]{0:T(128)S(6)} %copy.7.bound_ref, f32[512,1024]{1,0:T(8,128)} %bitcast.7), custom_call_target="tpu_custom_call" | custom-call | tf_op jit(solution)/shard_map/clipped_sum/pallas_call | solution.py:404
  97.0 1.3 %copy.6 = f32[1,512,1024]{2,1,0:T(8,128)} copy(f32[1,512,1024]{2,1,0:T(8,128)S(1)} %bitcast.4) | data formatting | bytes 4194304

commit v3 on v2

--- a/solution.py
+++ b/solution.py
@@ -158,7 +158,7 @@
             device_id={"mp": lax.rem(lane + j, lanes)}, device_id_type=MESH,
         )
 
-    for j in range(1, lanes):
+    for j in sorted(range(1, lanes), key=lambda j: -(j % 2 == 0)):
         norm_copy(j).start()
 
     def turn_step(e, carry):
@@ -212,7 +212,7 @@
     noise_copy = pltpu.make_async_copy(noise_hbm, noise, noise_sem)
     noise_copy.start()
     for j in range(1, lanes):
-        norm_copy(j).wait()
+        norm_copy(j).wait_recv()
 
     bound = bound_ref[0]
 
@@ -363,8 +363,6 @@
         out[:, cols_of(q)] = summed * out_factor + noise[:, cols_of(q)]
         return carry
 
-    lax.fori_loop(0, PIECES, final_step, 0)
-
     def drain_step(s, carry):
         t, q = s // PIECES, s % PIECES
         far = is_far(t, q)
@@ -383,10 +381,17 @@
 
         return carry
 
-    lax.fori_loop(0, planes * PIECES, drain_step, 0)
-    if share > 1:
-        for i in range(owned):
-            gram_copy(i).wait_send()
+    def drain():
+        lax.fori_loop(0, planes * PIECES, drain_step, 0)
+        for j in range(1, lanes):
+            norm_copy(j).wait_send()
+        if share > 1:
+            for i in range(owned):
+                gram_copy(i).wait_send()
+
+    lax.fori_loop(0, PIECES - 1, final_step, 0)
+    drain()
+    final_step(PIECES - 1, 0)
 
 
 def clipped_sum(act_block, grad_block, bound, noise, out_factor):

time: 98.5 us -> 98.2 us (level)
  no operation moved by 1% of the time
where the time goes in v3:
time: 98.2 us; the launch traced here: 98.1 us
  Pallas kernels  96.1 us (98%)
  local copies, waits for them, and re-layouts  1.32 us (1%)
    pallas_call x1, Pallas kernels, clipped_sum(): pl.pallas_call(functools.partial(kernel, groups, lanes, share, out_factor...  96.1 us

profile of v3, /device:TPU:0, one launch (start us, length us, event | category | flops | bytes accessed | tf_op | source)
XLA Modules:
  0.0 98.1 jit_solution(6479383271889290688)
XLA Ops:
  0.7 96.1 %clipped_sum.1 = f32[512,1024]{1,0:T(8,128)S(1)} custom-call(bf16[2048,4096]{1,0:T(8,128)(2,1)} %bitcast.5, bf16[2048,1024]{1,0:T(8,128)(2,1)} %bitcast.6, f32[1]{0:T(128)S(6)} %copy.7.bound_ref, f32[512,1024]{1,0:T(8,128)} %bitcast.7), custom_call_target="tpu_custom_call" | custom-call | tf_op jit(solution)/shard_map/clipped_sum/pallas_call | solution.py:409
  96.7 1.3 %copy.6 = f32[1,512,1024]{2,1,0:T(8,128)} copy(f32[1,512,1024]{2,1,0:T(8,128)S(1)} %bitcast.4) | data formatting | bytes 4194304
